TPU v7x, 32 devices: a whole 2x2x4 slice. The times are simulated.
32 devices in a mesh: fsdp: 4 (over y, x), rep: 8 (over z, core).
Axes of the slice: x: 2, y: 2, z: 4, core: 2. Of those that a mesh axis runs over, the one named last changes fastest.
Arguments:
- inputs: bfloat16 [64, 128, 2048], P(('fsdp', 'rep')), may hold values from -6 to 6
- segment_ids: int32 [64, 128], P(('fsdp', 'rep')), may hold values from 0 to 3, never falling along the last dimension, each value on 1 to 64 neighbouring positions
- cotangent: bfloat16 [64, 128, 2048], P(('fsdp', 'rep')), may hold values from -6 to 6
- norm_gain: bfloat16 [2048], replicated, may hold values from 0.5 to 1.5
- norm_shift: bfloat16 [2048], replicated, may hold values from -4 to 4
- qkv_weight: bfloat16 [2048, 6144], P('fsdp'), may hold values from -0.125 to 0.125
- qkv_bias: bfloat16 [6144], replicated, may hold values from -6 to 6
- dense_weight: bfloat16 [2048, 2048], P('fsdp'), may hold values from -0.375 to 0.375
- dense_bias: bfloat16 [2048], replicated, may hold values from -4 to 4
- fc1_weight: bfloat16 [2048, 8192], P('fsdp'), may hold values from -0.125 to 0.125
- fc1_bias: bfloat16 [8192], replicated, may hold values from -6 to 6
- fc2_weight: bfloat16 [8192, 2048], P('fsdp'), may hold values from -0.125 to 0.125
- fc2_bias: bfloat16 [2048], replicated, may hold values from -4 to 4
Outputs:
- layer_output: bfloat16 [64, 128, 2048], P(('fsdp', 'rep'))
- input_grad: bfloat16 [64, 128, 2048], P(('fsdp', 'rep'))
- norm_gain_grad: float32 [2048], P('fsdp')
- norm_shift_grad: float32 [2048], P('fsdp')
- qkv_weight_grad: float32 [2048, 6144], P('fsdp')
- qkv_bias_grad: float32 [6144], P('fsdp')
- dense_weight_grad: float32 [2048, 2048], P('fsdp')
- dense_bias_grad: float32 [2048], P('fsdp')
- fc1_weight_grad: float32 [2048, 8192], P('fsdp')
- fc1_bias_grad: float32 [8192], P('fsdp')
- fc2_weight_grad: float32 [8192, 2048], P('fsdp')
- fc2_bias_grad: float32 [2048], P('fsdp')
Inputs may be any that keep to these rules, and one draw needn't show every extreme that they name: `segment_ids`: along each sequence the document numbers never fall; every document has 1 to 64 tokens, and some document has exactly 64.
All inputs are finite; a program needn't handle non-finite values.
Results may differ from a plain program's by a relative error of at most 0.015.
Values may be sent and summed in bfloat16 or wider, within the bound.
A program may use at most 832 MiB of HBM per device.

v0:
```python
from functools import partial
import jax
import jax.numpy as jnp
from jax import lax
from jax.sharding import PartitionSpec as P

HEADS = 32
HD = 64
ROT = 32
norm_eps = 1e-05


def positions_of(segment_row):
    last_axis = segment_row.ndim - 1
    token_index = lax.broadcasted_iota(jnp.int32, segment_row.shape, last_axis)
    previous = jnp.concatenate([segment_row[..., :1] - 1, segment_row[..., :-1]], axis=last_axis)
    starts = jnp.where(segment_row != previous, token_index, 0)
    return token_index - lax.cummax(starts, axis=last_axis)


def rotary_tables(positions):
    half_rot = ROT // 2
    inv_freq = 10000.0 ** (-2.0 * jnp.arange(half_rot, dtype=jnp.float32) / ROT)
    angles = positions.astype(jnp.float32)[..., None] * inv_freq
    angles = jnp.concatenate([angles, angles], axis=-1)
    return (jnp.cos(angles), jnp.sin(angles))


def rotate(values, cos_tab, sine_tab):
    half_rot = ROT // 2
    turned = values[..., :ROT]
    swapped = jnp.concatenate([-turned[..., half_rot:], turned[..., :half_rot]], axis=-1)
    turned = turned * cos_tab[:, None, :] + swapped * sine_tab[:, None, :]
    return jnp.concatenate([turned, values[..., ROT:]], axis=-1)


def rotate_back(grad_in, cos_tab, sine_tab):
    half_rot = ROT // 2
    rot_part = grad_in[..., :ROT]
    scaled = rot_part * sine_tab[:, None, :]
    rot_back = jnp.concatenate([scaled[..., half_rot:], -scaled[..., :half_rot]], axis=-1)
    rot_part = rot_part * cos_tab[:, None, :] + rot_back
    return jnp.concatenate([rot_part, grad_in[..., ROT:]], axis=-1)


def dot_last(left_op, right_op):
    return lax.dot_general(
        left_op, right_op, (((1,), (1,)), ((), ())), preferred_element_type=jnp.float32
    )


def dot_first(left_op, right_op):
    return lax.dot_general(
        left_op, right_op, (((0,), (0,)), ((), ())), preferred_element_type=jnp.float32
    )


def row_adder(left_b):

    def add_rows(running, shard_rows, first_row):
        return jnp.dot(left_b, shard_rows, preferred_element_type=jnp.float32)

    return add_rows


def column_maker(back_b, shard_rows):
    return dot_last(back_b, shard_rows)


def gelu_back(pre_act, d_hidden):
    gelu_vals, pull_back = jax.vjp(partial(jax.nn.gelu, approximate=True), pre_act)
    return pull_back(d_hidden)[0]


def per_device(
    inputs,
    segment_ids,
    cotangent,
    norm_gain,
    norm_shift,
    qkv_weight,
    qkv_bias,
    dense_weight,
    dense_bias,
    fc1_weight,
    fc1_bias,
    fc2_weight,
    fc2_bias,
):
    micro_count, seq_len, model_width = inputs.shape
    ffn_width = fc1_weight.shape[1]
    score_scale = HD ** (-0.5)
    gain_f32 = norm_gain.astype(jnp.float32)
    shift_f32 = norm_shift.astype(jnp.float32)
    qkv_bias_f32 = qkv_bias.astype(jnp.float32)
    dense_bias_f32 = dense_bias.astype(jnp.float32)
    fc1_bias_f32 = fc1_bias.astype(jnp.float32)
    fc2_bias_f32 = fc2_bias.astype(jnp.float32)
    token_index = jnp.arange(seq_len, dtype=jnp.int32)
    causal = token_index[:, None] >= token_index[None, :]
    layer_outs = []
    input_grads = []
    kept_normed = []
    kept_joined = []
    kept_pre = []
    kept_mixed = []
    kept_hidden = []
    kept_back = []
    gain_sum = jnp.zeros((model_width,), jnp.float32)
    shift_sum = jnp.zeros((model_width,), jnp.float32)
    qkv_bias_sum = jnp.zeros((3 * model_width,), jnp.float32)
    back_sum = jnp.zeros((model_width,), jnp.float32)
    fc1_bias_sum = jnp.zeros((ffn_width,), jnp.float32)
    for micro_step in range(micro_count):
        token_rows = inputs[micro_step].astype(jnp.float32)
        segment_row = segment_ids[micro_step]
        row_mean = jnp.mean(token_rows, axis=-1, keepdims=True)
        centred = token_rows - row_mean
        row_var = jnp.mean(centred * centred, axis=-1, keepdims=True)
        inv_std = lax.rsqrt(row_var + norm_eps)
        x_hat = centred * inv_std
        normed = (x_hat * gain_f32 + shift_f32).astype(jnp.bfloat16)
        add_normed = row_adder(normed)
        start_sums = (
            jnp.zeros((seq_len, 3 * model_width), jnp.float32),
            jnp.zeros((seq_len, ffn_width), jnp.float32),
        )
        add_first_row = jnp.int32(0)
        joined_qkv = add_normed(
            start_sums[0], lax.all_gather(qkv_weight, "fsdp", axis=0, tiled=True), add_first_row
        )
        pre_act = add_normed(
            start_sums[1], lax.all_gather(fc1_weight, "fsdp", axis=0, tiled=True), add_first_row
        )
        joined_qkv = joined_qkv + qkv_bias_f32
        pre_act = pre_act + fc1_bias_f32
        hidden_b = jax.nn.gelu(pre_act, approximate=True).astype(jnp.bfloat16)
        cos_tab, sine_tab = rotary_tables(positions_of(segment_row))
        joined_heads = joined_qkv.reshape(seq_len, 3, HEADS, HD)
        query_b = rotate(joined_heads[:, 0], cos_tab, sine_tab).astype(jnp.bfloat16)
        key_b = rotate(joined_heads[:, 1], cos_tab, sine_tab).astype(jnp.bfloat16)
        value_b = joined_heads[:, 2].astype(jnp.bfloat16)
        allowed = causal & (segment_row[:, None] == segment_row[None, :])
        scores = (
            jnp.einsum("qhd,khd->hqk", query_b, key_b, preferred_element_type=jnp.float32)
            * score_scale
        )
        scores = jnp.where(allowed[None], scores, -1e30)
        row_max = jnp.max(scores, axis=-1, keepdims=True)
        exp_scores = jnp.exp(scores - row_max)
        row_total = jnp.sum(exp_scores, axis=-1, keepdims=True)
        probs_b = (exp_scores / row_total).astype(jnp.bfloat16)
        log_total = row_max + jnp.log(row_total)
        mixed_b = jnp.einsum("hqk,khd->qhd", probs_b, value_b, preferred_element_type=jnp.float32)
        mixed_b = mixed_b.reshape(seq_len, model_width).astype(jnp.bfloat16)
        start_out = jnp.zeros((seq_len, model_width), jnp.float32)
        attn_out = row_adder(mixed_b)(
            start_out, lax.all_gather(dense_weight, "fsdp", axis=0, tiled=True), jnp.int32(0)
        )
        mlp_out = row_adder(hidden_b)(
            start_out, lax.all_gather(fc2_weight, "fsdp", axis=0, tiled=True), jnp.int32(0)
        )
        layer_outs.append(
            (token_rows + attn_out + dense_bias_f32 + mlp_out + fc2_bias_f32).astype(jnp.bfloat16)
        )
        back_b = cotangent[micro_step]
        back_f32 = back_b.astype(jnp.float32)
        back_sum = back_sum + jnp.sum(back_f32, axis=0)
        d_mixed = column_maker(back_b, lax.all_gather(dense_weight, "fsdp", axis=0, tiled=True))
        d_hidden = column_maker(back_b, lax.all_gather(fc2_weight, "fsdp", axis=0, tiled=True))
        d_mixed_b = d_mixed.astype(jnp.bfloat16).reshape(seq_len, HEADS, HD)
        d_pre_b = gelu_back(pre_act, d_hidden).astype(jnp.bfloat16)
        fc1_bias_sum = fc1_bias_sum + jnp.sum(d_pre_b, axis=0, dtype=jnp.float32)
        again_scores = (
            jnp.einsum("qhd,khd->hqk", query_b, key_b, preferred_element_type=jnp.float32)
            * score_scale
        )
        again_scores = jnp.where(allowed[None], again_scores, -1e30)
        attn_probs = jnp.exp(again_scores - log_total)
        d_probs = jnp.einsum("qhd,khd->hqk", d_mixed_b, value_b, preferred_element_type=jnp.float32)
        d_value = jnp.einsum(
            "hqk,qhd->khd",
            attn_probs.astype(jnp.bfloat16),
            d_mixed_b,
            preferred_element_type=jnp.float32,
        )
        d_scores_b = (
            attn_probs * (d_probs - jnp.sum(attn_probs * d_probs, axis=-1, keepdims=True))
        ).astype(jnp.bfloat16)
        d_query = (
            jnp.einsum("hqk,khd->qhd", d_scores_b, key_b, preferred_element_type=jnp.float32)
            * score_scale
        )
        d_key = (
            jnp.einsum("hqk,qhd->khd", d_scores_b, query_b, preferred_element_type=jnp.float32)
            * score_scale
        )
        d_query = rotate_back(d_query, cos_tab, sine_tab)
        d_key = rotate_back(d_key, cos_tab, sine_tab)
        d_joined_b = (
            jnp.stack([d_query, d_key, d_value], axis=1)
            .reshape(seq_len, 3 * model_width)
            .astype(jnp.bfloat16)
        )
        qkv_bias_sum = qkv_bias_sum + jnp.sum(d_joined_b, axis=0, dtype=jnp.float32)
        block_cols = dot_last(
            d_joined_b, lax.all_gather(qkv_weight, "fsdp", axis=0, tiled=True)
        ) + dot_last(d_pre_b, lax.all_gather(fc1_weight, "fsdp", axis=0, tiled=True))
        gain_sum = gain_sum + jnp.sum(block_cols * x_hat, axis=0)
        shift_sum = shift_sum + jnp.sum(block_cols, axis=0)
        d_hat = block_cols * gain_f32
        d_input = inv_std * (
            d_hat
            - jnp.mean(d_hat, axis=-1, keepdims=True)
            - x_hat * jnp.mean(d_hat * x_hat, axis=-1, keepdims=True)
        )
        input_grads.append((back_f32 + d_input).astype(jnp.bfloat16))
        kept_normed.append(normed)
        kept_joined.append(d_joined_b)
        kept_pre.append(d_pre_b)
        kept_mixed.append(mixed_b)
        kept_hidden.append(hidden_b)
        kept_back.append(back_b)
    normed_all = jnp.concatenate(kept_normed, axis=0)
    joined_all = jnp.concatenate(kept_joined, axis=0)
    pre_all = jnp.concatenate(kept_pre, axis=0)
    mixed_all = jnp.concatenate(kept_mixed, axis=0)
    hidden_all = jnp.concatenate(kept_hidden, axis=0)
    back_all = jnp.concatenate(kept_back, axis=0)
    dense_rows = dense_weight.shape[0]
    fc2_rows = fc2_weight.shape[0]
    block_rows = dense_rows + fc2_rows
    first_rows = lax.psum_scatter(
        jnp.concatenate(
            [dot_first(normed_all, joined_all), dot_first(normed_all, pre_all)], axis=1
        ).astype(jnp.bfloat16),
        "fsdp",
        scatter_dimension=0,
        tiled=True,
    )
    first_row = jnp.int32(0)
    collected = []
    for offset in range(block_rows * lax.axis_size("fsdp") // block_rows):
        owner_idx = first_row // block_rows + offset
        mixed_cols = lax.dynamic_slice_in_dim(mixed_all, owner_idx * dense_rows, dense_rows, 1)
        hid_cols = lax.dynamic_slice_in_dim(hidden_all, owner_idx * fc2_rows, fc2_rows, 1)
        collected.append(dot_first(mixed_cols, back_all))
        collected.append(dot_first(hid_cols, back_all))
    second_rows = lax.psum_scatter(
        jnp.concatenate(collected, axis=0).astype(jnp.bfloat16),
        "fsdp",
        scatter_dimension=0,
        tiled=True,
    )
    small_sums = (
        lax.psum_scatter(
            gain_sum.astype(jnp.bfloat16), "fsdp", scatter_dimension=0, tiled=True
        ).astype(jnp.float32),
        lax.psum_scatter(
            shift_sum.astype(jnp.bfloat16), "fsdp", scatter_dimension=0, tiled=True
        ).astype(jnp.float32),
        lax.psum_scatter(
            qkv_bias_sum.astype(jnp.bfloat16), "fsdp", scatter_dimension=0, tiled=True
        ).astype(jnp.float32),
        lax.psum_scatter(
            back_sum.astype(jnp.bfloat16), "fsdp", scatter_dimension=0, tiled=True
        ).astype(jnp.float32),
        lax.psum_scatter(
            fc1_bias_sum.astype(jnp.bfloat16), "fsdp", scatter_dimension=0, tiled=True
        ).astype(jnp.float32),
    )
    totals = (
        lax.psum(first_rows, "rep").astype(jnp.float32),
        lax.psum(second_rows, "rep").astype(jnp.float32),
        lax.psum(small_sums[0].astype(jnp.bfloat16), "rep").astype(jnp.float32),
        lax.psum(small_sums[1].astype(jnp.bfloat16), "rep").astype(jnp.float32),
        lax.psum(small_sums[2].astype(jnp.bfloat16), "rep").astype(jnp.float32),
        lax.psum(small_sums[3].astype(jnp.bfloat16), "rep").astype(jnp.float32),
        lax.psum(small_sums[4].astype(jnp.bfloat16), "rep").astype(jnp.float32),
    )
    first_total = totals[0]
    second_total = totals[1]
    return (
        jnp.stack(layer_outs, axis=0),
        jnp.stack(input_grads, axis=0),
        totals[2],
        totals[3],
        first_total[:, : 3 * model_width],
        totals[4],
        second_total[:dense_rows],
        totals[5],
        first_total[:, 3 * model_width :],
        totals[6],
        second_total[dense_rows:],
        totals[5],
    )


def solution(mesh):
    placed = (
        P(("fsdp", "rep"), None, None),
        P(("fsdp", "rep"), None),
        P(("fsdp", "rep"), None, None),
        P(),
        P(),
        P("fsdp", None),
        P(),
        P("fsdp", None),
        P(),
        P("fsdp", None),
        P(),
        P("fsdp", None),
        P(),
    )
    return jax.shard_map(
        per_device,
        mesh=mesh,
        in_specs=placed,
        out_specs=(
            P(("fsdp", "rep"), None, None),
            P(("fsdp", "rep"), None, None),
            P("fsdp"),
            P("fsdp"),
            P("fsdp", None),
            P("fsdp"),
            P("fsdp", None),
            P("fsdp"),
            P("fsdp", None),
            P("fsdp"),
            P("fsdp", None),
            P("fsdp"),
        ),
        check_vma=False,
    )
```

profile of v0, /device:TPU:0, one launch (start us, length us, event | category | flops | bytes accessed | tf_op | source)
XLA Modules:
  0.0 2319.4 jit_solution(13919648007534341312)
XLA Ops:
  17.1 223.1 %all-gather.5.cloned.1.call-done = bf16[2048,6144]{1,0:T(8,128)(2,1)} async-done(((bf16[512,6144]{1,0:T(8,128)(2,1)}), bf16[2048,6144]{1,0:T(8,128)(2,1)}) %all-gather.5.cloned.1.call-update) | async-done | bytes 25165840 | tf_op jit(solution)/shard_map/all_gather | solution.py:130
  240.2 10.5 convolution_add_fusion.3
  257.7 13.4 convolution_add_fusion.2
  285.0 254.1 %all-gather.9.cloned.1.call-done = bf16[2048,8192]{1,0:T(8,128)(2,1)} async-done(((bf16[512,8192]{1,0:T(8,128)(2,1)}), bf16[2048,8192]{1,0:T(8,128)(2,1)}) %all-gather.9.cloned.1.call-update) | async-done | bytes 33554448 | tf_op jit(solution)/shard_map/all_gather | solution.py:133
  539.1 17.8 multiply_convert_fusion.1
  557.0 16.7 multiply_convert_fusion
  596.9 5.7 convert_dynamic-update-slice_fusion
  602.9 25.6 %all-gather.7.cloned.1.call-done = bf16[2048,2048]{1,0:T(8,128)(2,1)} async-done(((bf16[512,2048]{1,0:T(8,128)(2,1)}), bf16[2048,2048]{1,0:T(8,128)(2,1)}) %all-gather.7.cloned.1.call-update) | async-done | bytes 8388624 | tf_op jit(solution)/shard_map/all_gather | solution.py:158
  628.5 7.1 convolution_convert_fusion.6
  637.7 10.0 convolution_convert_fusion.7
  664.6 13.2 convolution_convert_fusion.1
  677.8 249.5 %all-gather.11.cloned.1.call-done = bf16[8192,2048]{1,0:T(8,128)(2,1)} async-done(((bf16[2048,2048]{1,0:T(8,128)(2,1)}), bf16[8192,2048]{1,0:T(8,128)(2,1)}) %all-gather.11.cloned.1.call-update) | async-done | bytes 33554448 | tf_op jit(solution)/shard_map/all_gather | solution.py:161
  927.3 19.3 convert_reduce_fusion.1
  946.6 19.7 convert_reduce_fusion
  966.3 17.0 convolution_convert_fusion
  983.3 40.6 %pad_maximum_fusion = bf16[2048,14336]{1,0:T(8,128)(2,1)} fusion(bf16[2048,8192]{1,0:T(8,128)(2,1)} %convolution_convert_fusion, bf16[2048,6144]{1,0:T(8,128)(2,1)} %convolution_convert_fusion.1), kind=kLoop, calls=%fused_computation | loop fusion | flops 117440512 | bytes 117440512 | tf_op jit(solution)/shard_map/concatenate | solution.py:234
  1027.3 6.0 fusion.26
  1033.4 6.0 fusion.27
  1039.4 14.7 fusion.137
  1054.0 232.5 %reduce-scatter.7.cloned.1.call-done = bf16[2560,2048]{1,0:T(8,128)(2,1)} async-done(((bf16[10240,2048]{1,0:T(8,128)(2,1)}), bf16[2560,2048]{1,0:T(8,128)(2,1)}) %reduce-scatter.7.cloned.1.call-update) | async-done | bytes 10485776
  1286.6 494.7 %reduce-scatter.5.cloned.1.call-done = bf16[512,14336]{1,0:T(8,128)(2,1)} async-done(((bf16[2048,14336]{1,0:T(8,128)(2,1)}), bf16[512,14336]{1,0:T(8,128)(2,1)}) %reduce-scatter.5.cloned.1.call-update) | async-done | bytes 14680080 | tf_op jit(solution)/shard_map/reduce_scatter | solution.py:233
  1781.2 14.2 fusion.138
  1795.4 17.0 convolution_add_fusion.4
  1812.5 19.8 fusion.66
  1835.7 15.9 all-reduce.8
  1851.9 27.9 %all-reduce.6 = (bf16[512]{0:T(512)(128)(2,1)S(1)}, bf16[512]{0:T(512)(128)(2,1)S(1)}, bf16[1536]{0:T(1024)(128)(2,1)S(1)}, bf16[512]{0:T(512)(128)(2,1)S(1)}, bf16[2048]{0:T(1024)(128)(2,1)S(1)}) all-reduce(bf16[512]{0:T(512)(128)(2,1)S(1)} %dynamic-slice.1, ...), channel_id=1, replica_groups=mesh['fsdp'=4,'rep'=8] {'rep'}, use_global_device_ids=true, to_apply=%region_19.20 | all-reduce | flops 5120 | bytes 20480 | tf_op jit(solution)/shard_map/psum | solution.py:275
  1882.2 16.4 fusion.31
  1898.6 14.2 fusion.30
  1914.9 360.0 %all-reduce.11.cloned.1.call-done = (bf16[512,14336]{1,0:T(8,128)(2,1)}, bf16[2560,2048]{1,0:T(8,128)(2,1)}) async-done(((bf16[512,14336]{1,0:T(8,128)(2,1)}, bf16[2560,2048]{1,0:T(8,128)(2,1)}), (bf16[512,14336]{1,0:T(8,128)(2,1)}, bf16[2560,2048]{1,0:T(8,128)(2,1)})) %all-reduce.11.cloned.1.call-update) | async-done | bytes 25165840 | tf_op jit(solution)/shard_map/psum | solution.py:273
  2279.1 11.7 slice.279
  2290.8 9.2 slice.276
  2300.0 11.7 slice.278
  (258 shorter events, 85.4 us)
Async XLA Ops:
  7.2 233.0 %all-gather.5.cloned.1.call-start = ((), (), s32[]{:S(2)}) async-start(), calls=%async_computation.2 | async-start | bytes 31457280 | tf_op jit(solution)/shard_map/all_gather | solution.py:130
  7.9 531.2 %all-gather.9.cloned.1.call-start = ((), (), s32[]{:S(2)}) async-start(), calls=%async_computation.4 | async-start | bytes 41943040 | tf_op jit(solution)/shard_map/all_gather | solution.py:133
  8.7 619.8 %all-gather.7.cloned.1.call-start = ((), (), s32[]{:S(2)}) async-start(), calls=%async_computation.3 | async-start | bytes 10485760 | tf_op jit(solution)/shard_map/all_gather | solution.py:158
  9.5 917.8 %all-gather.11.cloned.1.call-start = ((), (), s32[]{:S(2)}) async-start(), calls=%async_computation.5 | async-start | bytes 41943040 | tf_op jit(solution)/shard_map/all_gather | solution.py:161
  10.0 1276.5 %reduce-scatter.7.cloned.1.call-start = ((), (), s32[]{:S(2)}) async-start(), calls=%async_computation.7 | async-start | bytes 52428800
  12.0 238.7 %copy-start.47 = (f32[2048]{0:T(1024)}, f32[2048]{0:T(1024)S(1)}, u32[]{:S(2)}) copy-start(f32[2048]{0:T(1024)S(1)} %convert_element_type.215) | copy-start | bytes 24580
  13.9 236.8 %copy-start.52 = (f32[128]{0:T(128)}, f32[128]{0:T(128)S(1)}, u32[]{:S(2)}) copy-start(f32[128]{0:T(128)S(1)} %get-tuple-element.123) | copy-start | bytes 1540
  13.9 236.8 %copy-start.54 = (f32[128]{0:T(128)}, f32[128]{0:T(128)S(1)}, u32[]{:S(2)}) copy-start(f32[128]{0:T(128)S(1)} %get-tuple-element.124) | copy-start | bytes 1540
  14.4 236.3 %copy-start.58 = (f32[128]{0:T(128)}, f32[128]{0:T(128)S(1)}, u32[]{:S(2)}) copy-start(f32[128]{0:T(128)S(1)} %add_rsqrt_fusion.1) | copy-start | bytes 1540
  14.4 236.3 %copy-start.60 = (f32[128]{0:T(128)}, f32[128]{0:T(128)S(1)}, u32[]{:S(2)}) copy-start(f32[128]{0:T(128)S(1)} %add_rsqrt_fusion) | copy-start | bytes 1540
  282.2 257.0 %copy-start.8 = (bf16[128,2048]{1,0:T(8,128)(2,1)S(1)}, bf16[128,2048]{1,0:T(8,128)(2,1)}, u32[]{:S(2)}) copy-start(bf16[128,2048]{1,0:T(8,128)(2,1)} %get-tuple-element.50) | copy-start | bytes 1572868
  285.0 271.9 %copy-start.11 = (bf16[128,2048]{1,0:T(8,128)(2,1)S(1)}, bf16[128,2048]{1,0:T(8,128)(2,1)}, u32[]{:S(2)}) copy-start(bf16[128,2048]{1,0:T(8,128)(2,1)} %get-tuple-element.51) | copy-start | bytes 1572868
  539.1 17.8 copy-start.49
  557.0 40.0 %copy-start.20 = (bf16[128,8192]{1,0:T(8,128)(2,1)}, bf16[128,8192]{1,0:T(8,128)(2,1)S(1)}, u32[]{:S(2)}) copy-start(bf16[128,8192]{1,0:T(8,128)(2,1)S(1)} %get-tuple-element.112) | copy-start | bytes 6291460
  557.0 16.7 copy-start.44
  557.0 16.7 copy-start.46
  573.7 23.2 %copy-start.18 = (bf16[128,8192]{1,0:T(8,128)(2,1)}, bf16[128,8192]{1,0:T(8,128)(2,1)S(1)}, u32[]{:S(2)}) copy-start(bf16[128,8192]{1,0:T(8,128)(2,1)S(1)} %get-tuple-element.108) | copy-start | bytes 6291460
  602.6 25.9 %copy-start.5 = (bf16[2,128,2048]{2,1,0:T(8,128)(2,1)S(1)}, bf16[2,128,2048]{2,1,0:T(8,128)(2,1)}, u32[]{:S(2)}) copy-start(bf16[2,128,2048]{2,1,0:T(8,128)(2,1)} %param.15) | copy-start | bytes 3145732
  602.7 1178.6 %reduce-scatter.5.cloned.1.call-start = ((), (), s32[]{:S(2)}) async-start(), calls=%async_computation.6 | async-start | bytes 73400320 | tf_op jit(solution)/shard_map/reduce_scatter | solution.py:233
  664.6 262.7 %copy-start.6 = (bf16[2,128,2048]{2,1,0:T(8,128)(2,1)S(1)}, bf16[2,128,2048]{2,1,0:T(8,128)(2,1)}, u32[]{:S(2)}) copy-start(bf16[2,128,2048]{2,1,0:T(8,128)(2,1)} %param.15) | copy-start | bytes 3145732
  1024.1 1250.9 %all-reduce.11.cloned.1.call-start = ((), (), s32[]{:S(2)}) async-start(), calls=%async_computation.8 | async-start | bytes 50331648 | tf_op jit(solution)/shard_map/psum | solution.py:273
  1795.4 17.0 copy-start.48
  1795.4 17.0 copy-start.53
  1795.4 17.0 copy-start.55
  1795.4 17.0 copy-start.59
  1795.4 17.0 copy-start.61
  1812.5 19.8 copy-start.7
  1880.4 431.4 %copy-start.57 = (f32[512]{0:T(512)}, f32[512]{0:T(512)S(1)}, u32[]{:S(2)}) copy-start(f32[512]{0:T(512)S(1)} %convert_element_type.269) | copy-start | bytes 6148
  1882.2 16.4 copy-start.17
  1882.2 16.4 copy-start.19
  1898.6 15.3 copy-start.21
  1898.6 15.3 copy-start.22
  (42 other events, 111.3 us)
Sparse Core Ops, SparseCore 0:
  9.9 230.2 all-gather.4
  242.0 297.0 all-gather.8
  541.0 87.4 all-gather.6
  630.2 297.0 all-gather.10
  930.3 356.2 reduce-scatter.6
  1289.5 491.6 reduce-scatter.4
  1783.8 491.0 all-reduce.10
where the time goes:
time: 2320 us
  waiting for transfers between devices  1840 us (79%)
  matrix products  297 us (13%)
  other arithmetic  59.1 us (3%)
  local copies, waits for them, and re-layouts  57.9 us (2%)
  blocking collectives  43.8 us (2%)
    reduce_scatter x1, waiting for transfers between devices, per_device(): lax.psum_scatter(jnp.concatenate([dot_first(normed_all, joined_all), dot_...  495 us
    psum x1, waiting for transfers between devices, per_device(): lax.psum(first_rows, 'rep').astype(jnp.float32)  360 us
    all_gather x1, waiting for transfers between devices, per_device(): lax.all_gather(fc1_weight, 'fsdp', axis=0, tiled=True)  254 us
    all_gather x1, waiting for transfers between devices, per_device(): lax.all_gather(fc2_weight, 'fsdp', axis=0, tiled=True)  249 us
    unnamed x8, waiting for transfers between devices  235 us
    all_gather x1, waiting for transfers between devices, per_device(): lax.all_gather(qkv_weight, 'fsdp', axis=0, tiled=True)  223 us
    dot_general x8, matrix products, dot_last(): lax.dot_general(left_op, right_op, (((1,), (1,)), ((), ())), preferred_el...  122 us
    dot_general x8, matrix products, add_rows(): return jnp.dot(left_b, shard_rows, preferred_element_type=jnp.float32)  101 us
  transfers between devices with their start and end apart: 7, of which 7 were waited for; matrix products, arithmetic and copies ran while one was open for 16% of the time, Pallas kernels for 0%

commit v1 on v0

--- a/solution.py
+++ b/solution.py
@@ -8,6 +8,10 @@
 HD = 64
 ROT = 32
 norm_eps = 1e-05
+
+
+def render_the_body(z_in, peer_axis):
+    return lax.all_gather(z_in, peer_axis).sum(axis=0)
 
 
 def positions_of(segment_row):
@@ -270,7 +274,7 @@
         ).astype(jnp.float32),
     )
     totals = (
-        lax.psum(first_rows, "rep").astype(jnp.float32),
+        render_the_body(first_rows, "rep").astype(jnp.float32),
         lax.psum(second_rows, "rep").astype(jnp.float32),
         lax.psum(small_sums[0].astype(jnp.bfloat16), "rep").astype(jnp.float32),
         lax.psum(small_sums[1].astype(jnp.bfloat16), "rep").astype(jnp.float32),

time: 2320 us -> 3060 us (1.32)
  waiting for transfers between devices: 1840 us -> 2530 us
  other arithmetic: 59.1 us -> 103 us
    all_gather x0 -> x1, waiting for transfers between devices: none -> 958 us  [render_the_body(): return lax.all_gather(z_in, peer_axis).sum(axis=0)]
    psum x1, waiting for transfers between devices: 360 us -> 55.2 us  [per_device(): lax.psum(second_rows, 'rep').astype(jnp.float32)]
    reduce_sum x0 -> x1, other arithmetic: none -> 44.4 us  [render_the_body(): return lax.all_gather(z_in, peer_axis).sum(axis=0)]
    unnamed x8 -> x9, waiting for transfers between devices: 235 us -> 265 us
  transfers between devices with their start and end apart: 7 -> 8, of which waited for: 7 -> 8; matrix products, arithmetic and copies ran while one was open for 16% -> 13% of each run, Pallas kernels for 0% -> 0%
where the time goes in v1:
time: 3060 us; the launch traced here: 3050 us
  waiting for transfers between devices  2530 us (83%)
  matrix products  297 us (10%)
  other arithmetic  103 us (3%)
  local copies, waits for them, and re-layouts  64.3 us (2%)
  blocking collectives  43.2 us (1%)
    all_gather x1, waiting for transfers between devices, render_the_body(): return lax.all_gather(z_in, peer_axis).sum(axis=0)  958 us
    reduce_scatter x1, waiting for transfers between devices, per_device(): lax.psum_scatter(jnp.concatenate([dot_first(normed_all, joined_all), dot_...  495 us
    unnamed x9, waiting for transfers between devices  265 us
    all_gather x1, waiting for transfers between devices, per_device(): lax.all_gather(fc1_weight, 'fsdp', axis=0, tiled=True)  254 us
    all_gather x1, waiting for transfers between devices, per_device(): lax.all_gather(fc2_weight, 'fsdp', axis=0, tiled=True)  249 us
    all_gather x1, waiting for transfers between devices, per_device(): lax.all_gather(qkv_weight, 'fsdp', axis=0, tiled=True)  223 us
    dot_general x8, matrix products, dot_last(): lax.dot_general(left_op, right_op, (((1,), (1,)), ((), ())), preferred_el...  123 us
    dot_general x8, matrix products, add_rows(): return jnp.dot(left_b, shard_rows, preferred_element_type=jnp.float32)  99.4 us
  transfers between devices with their start and end apart: 8, of which 8 were waited for; matrix products, arithmetic and copies ran while one was open for 13% of the time, Pallas kernels for 0%

profile of v1, /device:TPU:0, one launch (start us, length us, event | category | flops | bytes accessed | tf_op | source)
XLA Modules:
  0.0 3052.0 jit_solution(5457248925414671754)
XLA Ops:
  17.0 223.1 %all-gather.7.cloned.1.call-done = bf16[2048,6144]{1,0:T(8,128)(2,1)} async-done(((bf16[512,6144]{1,0:T(8,128)(2,1)}), bf16[2048,6144]{1,0:T(8,128)(2,1)}) %all-gather.7.cloned.1.call-update) | async-done | bytes 25165840 | tf_op jit(solution)/shard_map/all_gather | solution.py:134
  240.2 10.5 convolution_add_fusion.2
  257.8 13.4 convolution_add_fusion.3
  285.0 254.1 %all-gather.11.cloned.1.call-done = bf16[2048,8192]{1,0:T(8,128)(2,1)} async-done(((bf16[512,8192]{1,0:T(8,128)(2,1)}), bf16[2048,8192]{1,0:T(8,128)(2,1)}) %all-gather.11.cloned.1.call-update) | async-done | bytes 33554448 | tf_op jit(solution)/shard_map/all_gather | solution.py:137
  539.1 17.6 multiply_convert_fusion
  556.8 16.7 multiply_convert_fusion.1
  596.6 5.7 convert_dynamic-update-slice_fusion
  602.6 26.0 all-gather.9.cloned.1.call-done
  628.6 7.1 convolution_convert_fusion.6
  637.8 10.0 convolution_convert_fusion.7
  665.5 13.2 convolution_convert_fusion.1
  678.7 248.7 %all-gather.13.cloned.1.call-done = bf16[8192,2048]{1,0:T(8,128)(2,1)} async-done(((bf16[2048,2048]{1,0:T(8,128)(2,1)}), bf16[8192,2048]{1,0:T(8,128)(2,1)}) %all-gather.13.cloned.1.call-update) | async-done | bytes 33554448 | tf_op jit(solution)/shard_map/all_gather | solution.py:165
  927.4 19.3 convert_reduce_fusion
  946.6 19.7 convert_reduce_fusion.1
  966.4 17.0 convolution_convert_fusion
  983.4 40.6 %pad_maximum_fusion = bf16[2048,14336]{1,0:T(8,128)(2,1)} fusion(bf16[2048,8192]{1,0:T(8,128)(2,1)} %convolution_convert_fusion, bf16[2048,6144]{1,0:T(8,128)(2,1)} %convolution_convert_fusion.1), kind=kLoop, calls=%fused_computation | loop fusion | flops 117440512 | bytes 117440512 | tf_op jit(solution)/shard_map/concatenate | solution.py:238
  1024.1 262.5 %reduce-scatter.7.cloned.1.call-done = bf16[2560,2048]{1,0:T(8,128)(2,1)} async-done(((bf16[10240,2048]{1,0:T(8,128)(2,1)}), bf16[2560,2048]{1,0:T(8,128)(2,1)}) %reduce-scatter.7.cloned.1.call-update) | async-done | bytes 10485776
  1286.7 494.6 %reduce-scatter.5.cloned.1.call-done = bf16[512,14336]{1,0:T(8,128)(2,1)} async-done(((bf16[2048,14336]{1,0:T(8,128)(2,1)}), bf16[512,14336]{1,0:T(8,128)(2,1)}) %reduce-scatter.5.cloned.1.call-update) | async-done | bytes 14680080 | tf_op jit(solution)/shard_map/reduce_scatter | solution.py:237
  1796.0 14.5 fusion.138
  1810.5 14.5 fusion.137
  1825.0 17.5 convolution_add_fusion.4
  1842.6 19.9 fusion.66
  1866.0 16.1 all-reduce.7
  1882.4 27.1 all-reduce.6
  1911.8 16.4 fusion.30
  1928.3 13.5 fusion.31
  1943.9 55.2 %all-reduce.10.cloned.1.call-done = bf16[2560,2048]{1,0:T(8,128)(2,1)} async-done(((bf16[2560,2048]{1,0:T(8,128)(2,1)}), bf16[2560,2048]{1,0:T(8,128)(2,1)}) %all-reduce.10.cloned.1.call-update) | async-done | bytes 10485776 | tf_op jit(solution)/shard_map/psum | solution.py:278
  2003.3 17.6 slice.279
  2020.8 958.1 %all-gather.15.cloned.1.call-done = bf16[4096,14336]{1,0:T(8,128)(2,1)} async-done(((bf16[512,14336]{1,0:T(8,128)(2,1)}), bf16[4096,14336]{1,0:T(8,128)(2,1)}) %all-gather.15.cloned.1.call-update) | async-done | bytes 117440528 | tf_op jit(solution)/shard_map/all_gather | solution.py:14
  2978.9 44.4 %reduce_sum.226 = bf16[512,14336]{1,0:T(8,128)(2,1)} reduce(bf16[8,512,14336]{2,1,0:T(8,128)(2,1)} %bitcast.42, bf16[]{:T(256)} %constant.116.clone.1), dimensions={0}, to_apply=%region_25.26 | reduce | flops 51380224 | bytes 132120576 | tf_op jit(solution)/shard_map/reduce_sum | solution.py:14
  3023.3 9.2 slice.276
  3032.6 11.7 slice.278
  (270 shorter events, 97.5 us)
Async XLA Ops:
  7.2 233.0 %all-gather.7.cloned.1.call-start = ((), (), s32[]{:S(2)}) async-start(), calls=%async_computation.2 | async-start | bytes 31457280 | tf_op jit(solution)/shard_map/all_gather | solution.py:134
  7.9 531.2 %all-gather.11.cloned.1.call-start = ((), (), s32[]{:S(2)}) async-start(), calls=%async_computation.4 | async-start | bytes 41943040 | tf_op jit(solution)/shard_map/all_gather | solution.py:137
  8.7 619.9 %all-gather.9.cloned.1.call-start = ((), (), s32[]{:S(2)}) async-start(), calls=%async_computation.3 | async-start | bytes 10485760 | tf_op jit(solution)/shard_map/all_gather | solution.py:162
  9.5 917.9 %all-gather.13.cloned.1.call-start = ((), (), s32[]{:S(2)}) async-start(), calls=%async_computation.5 | async-start | bytes 41943040 | tf_op jit(solution)/shard_map/all_gather | solution.py:165
  10.0 1276.6 %reduce-scatter.7.cloned.1.call-start = ((), (), s32[]{:S(2)}) async-start(), calls=%async_computation.9 | async-start | bytes 52428800
  10.1 240.6 %copy-start.51 = (f32[2048]{0:T(1024)}, f32[2048]{0:T(1024)S(1)}, u32[]{:S(2)}) copy-start(f32[2048]{0:T(1024)S(1)} %convert_element_type.217) | copy-start | bytes 24580
  13.9 236.8 %copy-start.56 = (f32[128]{0:T(128)}, f32[128]{0:T(128)S(1)}, u32[]{:S(2)}) copy-start(f32[128]{0:T(128)S(1)} %get-tuple-element.121) | copy-start | bytes 1540
  13.9 236.8 %copy-start.58 = (f32[128]{0:T(128)}, f32[128]{0:T(128)S(1)}, u32[]{:S(2)}) copy-start(f32[128]{0:T(128)S(1)} %get-tuple-element.122) | copy-start | bytes 1540
  14.4 236.3 %copy-start.62 = (f32[128]{0:T(128)}, f32[128]{0:T(128)S(1)}, u32[]{:S(2)}) copy-start(f32[128]{0:T(128)S(1)} %add_rsqrt_fusion.1) | copy-start | bytes 1540
  14.4 236.3 %copy-start.64 = (f32[128]{0:T(128)}, f32[128]{0:T(128)S(1)}, u32[]{:S(2)}) copy-start(f32[128]{0:T(128)S(1)} %add_rsqrt_fusion) | copy-start | bytes 1540
  282.2 257.0 %copy-start.13 = (bf16[128,2048]{1,0:T(8,128)(2,1)S(1)}, bf16[128,2048]{1,0:T(8,128)(2,1)}, u32[]{:S(2)}) copy-start(bf16[128,2048]{1,0:T(8,128)(2,1)} %get-tuple-element.49) | copy-start | bytes 1572868
  285.0 271.7 %copy-start.11 = (bf16[128,2048]{1,0:T(8,128)(2,1)S(1)}, bf16[128,2048]{1,0:T(8,128)(2,1)}, u32[]{:S(2)}) copy-start(bf16[128,2048]{1,0:T(8,128)(2,1)} %get-tuple-element.48) | copy-start | bytes 1572868
  539.1 17.6 copy-start.53
  556.7 39.8 %copy-start.24 = (bf16[128,8192]{1,0:T(8,128)(2,1)}, bf16[128,8192]{1,0:T(8,128)(2,1)S(1)}, u32[]{:S(2)}) copy-start(bf16[128,8192]{1,0:T(8,128)(2,1)S(1)} %get-tuple-element.106) | copy-start | bytes 6291460
  556.7 16.7 copy-start.48
  556.8 16.7 copy-start.50
  573.5 23.1 copy-start.22
  602.3 26.3 copy-start.6
  602.3 1178.9 %reduce-scatter.5.cloned.1.call-start = ((), (), s32[]{:S(2)}) async-start(), calls=%async_computation.6 | async-start | bytes 73400320 | tf_op jit(solution)/shard_map/reduce_scatter | solution.py:237
  665.5 261.9 %copy-start.7 = (bf16[2,128,2048]{2,1,0:T(8,128)(2,1)S(1)}, bf16[2,128,2048]{2,1,0:T(8,128)(2,1)}, u32[]{:S(2)}) copy-start(bf16[2,128,2048]{2,1,0:T(8,128)(2,1)} %param.15) | copy-start | bytes 3145732
  1024.1 975.1 %all-reduce.10.cloned.1.call-start = ((), (), s32[]{:S(2)}) async-start(), calls=%async_computation.7 | async-start | bytes 20971520 | tf_op jit(solution)/shard_map/psum | solution.py:278
  1286.7 1692.3 %all-gather.15.cloned.1.call-start = ((), (), s32[]{:S(2)}) async-start(), calls=%async_computation.8 | async-start | bytes 132120576 | tf_op jit(solution)/shard_map/all_gather | solution.py:14
  1825.0 17.5 copy-start.52
  1825.0 17.5 copy-start.57
  1825.0 17.5 copy-start.59
  1825.0 17.5 copy-start.63
  1825.0 17.5 copy-start.65
  1842.5 20.0 copy-start.8
  1842.6 20.0 copy-start.9
  1911.2 1133.1 %copy-start.61 = (f32[512]{0:T(512)}, f32[512]{0:T(512)S(1)}, u32[]{:S(2)}) copy-start(f32[512]{0:T(512)S(1)} %convert_element_type.271) | copy-start | bytes 6148
  1911.8 16.4 copy-start.21
  1911.8 16.4 copy-start.23
  (47 other events, 149.9 us)
Sparse Core Ops, SparseCore 0:
  9.9 230.2 all-gather.6
  242.0 297.0 all-gather.10
  541.0 87.5 all-gather.8
  630.3 297.0 all-gather.12
  930.3 356.2 reduce-scatter.6
  1289.6 491.6 reduce-scatter.4
  1783.6 215.4 all-reduce.9
  2000.8 978.1 all-gather.14
